TPU v7x, 512 devices: a 8x2x16 block of a 8x8x16 slice. The times are simulated.
512 devices in a mesh: groups: 2 (over y), tensor: 32 (over z, core), section: 8 (over x).
Axes of the slice: x: 8, y: 2, z: 16, core: 2. Of those that a mesh axis runs over, the one named last changes fastest.
The devices are a block of a 8x8x16 slice.
Arguments:
- hidden: bfloat16 [128, 8192], P('groups', 'tensor'), parts along dimension 0, may hold values from -6 to 6
- norm_gain: bfloat16 [8, 8192], P('section'), may hold values from 0.5 to 1.5
- query_weight: bfloat16 [8, 8192, 4096], P('section', None, 'tensor'), may hold values from -0.0625 to 0.0625
- query_bias: bfloat16 [8, 4096], P('section', 'tensor'), may hold values from -10 to 10
- kv_weight: bfloat16 [8, 8192, 1024], P('section', None, 'tensor'), may hold values from -0.0625 to 0.0625
- out_weight: bfloat16 [8, 4096, 8192], P('section', None, 'tensor'), may hold values from -0.09375 to 0.09375
- kv_pool: bfloat16 [8, 384, 16, 1024], P('section', ('groups', 'tensor')), parts along dimension 1, may hold values from -8 to 8
- page_table: int32 [128, 4], P(('groups', 'tensor')), parts along dimension 0, may hold values from 0 to 191, as said below
- context_len: int32 [128], P(('groups', 'tensor')), parts along dimension 0, may hold values from 33 to 64, as said below
Outputs:
- result: bfloat16 [128, 8192], P(('groups', 'section'), 'tensor'), parts along dimension 0
There are 2 independent parts, one for each index of `groups`. A program takes and returns all parts, laid end to end along the dimension named above; an argument that names none is the same for every part. Nothing has to cross between parts.
Inputs may be any that keep to these rules, and one draw needn't show every extreme that they name: `page_table`: sample r belongs to block k = r // 2; its 4 pages lie in k * 6 to (k + 1) * 6 - 1. The first 2 pages are the same for all samples of a block, every other page belongs to one sample only. `context_len`: some sample has 64 cached tokens.
All inputs are finite; a program needn't handle non-finite values.
Results may differ from a plain program's by a relative error of at most 0.018.
Values may be sent and summed in bfloat16 or wider, within the bound.
A program may use at most 64 MiB of HBM per device.

v0:
```python
import jax
import jax.numpy as jnp
from jax import lax
from jax.sharding import Mesh
from jax.sharding import PartitionSpec as P

HD = 128
KVH = 4
TENSOR = ("tensor_0", "tensor_1")
GROUPS_TENSOR = ("groups", "tensor_0", "tensor_1")
epsilon = 1e-06
rope_base = 1000000.0


def laid_out(tiles, dim):
    lengths = list(tiles.shape[1:])
    lengths[dim] *= tiles.shape[0]
    return jnp.moveaxis(tiles, 0, dim).reshape(lengths)


def all_blocks(shard, axes, turns):
    tiles = shard[None]
    for k in turns:
        tiles = lax.all_gather(tiles, axes[k], axis=0, tiled=True)
    block = [lax.axis_size(axes[k]) for k in reversed(turns)]
    tiles = tiles.reshape(*block, *shard.shape)
    turned = sorted(range(len(turns)), key=lambda place: turns[len(turns) - 1 - place])
    return tiles.transpose(*turned, *range(len(turns), tiles.ndim)).reshape(-1, *shard.shape)


def gathered_by_axis(shard, axes, turns, dim):
    return laid_out(all_blocks(shard, axes, turns), dim)


def shifted(value, axis, steps):
    count = lax.axis_size(axis)
    initial, last = (max(0, -steps), min(count, count - steps))
    return lax.ppermute(value, axis, [(source, source + steps) for source in range(initial, last)])


def rotate(values, position):
    head_size = values.shape[-1]
    half_size = head_size // 2
    frequency = rope_base ** (-(jnp.arange(half_size, dtype=jnp.float32) * 2.0) / head_size)
    angles = position.astype(jnp.float32)[:, None] * frequency[None, :]
    cosine = jnp.cos(angles)[:, None, :]
    sine_part = jnp.sin(angles)[:, None, :]
    front_half = values[..., :half_size]
    back_half = values[..., half_size:]
    return jnp.concatenate(
        [front_half * cosine - back_half * sine_part, back_half * cosine + front_half * sine_part],
        axis=-1,
    )


def attend(queries, key_new, value_new, cached, position):
    row_count, head_count, head_size = queries.shape
    kv_heads = key_new.shape[1]
    group_size = head_count // kv_heads
    span_len = cached.shape[1]
    keys_all = cached[:, :, : kv_heads * head_size].reshape(
        row_count, span_len, kv_heads, head_size
    )
    values_all = cached[:, :, kv_heads * head_size :].reshape(
        row_count, span_len, kv_heads, head_size
    )
    grouped = queries.reshape(row_count, kv_heads, group_size, head_size)
    scaling = head_size ** (-0.5)
    scores = (
        jnp.einsum("rkgd,rskd->rkgs", grouped, keys_all, preferred_element_type=jnp.float32)
        * scaling
    )
    own_score = (
        jnp.einsum("rkgd,rkd->rkg", grouped, key_new, preferred_element_type=jnp.float32) * scaling
    )
    usable = (jnp.arange(span_len, dtype=jnp.int32)[None, :] < position[:, None])[:, None, None, :]
    row_max = jnp.maximum(jnp.max(jnp.where(usable, scores, -1e30), axis=-1), own_score)
    weights = jnp.where(usable, jnp.exp(scores - row_max[..., None]), 0.0)
    own_weight = jnp.exp(own_score - row_max)
    denominator = jnp.sum(weights, axis=-1) + own_weight
    weights = (weights / denominator[..., None]).astype(jnp.bfloat16)
    own_weight = (own_weight / denominator).astype(jnp.bfloat16)
    mixture = jnp.einsum("rkgs,rskd->rkgd", weights, values_all, preferred_element_type=jnp.float32)
    mixture = (
        mixture
        + own_weight.astype(jnp.float32)[..., None] * value_new.astype(jnp.float32)[:, :, None, :]
    )
    return mixture.reshape(row_count, head_count * head_size).astype(jnp.bfloat16)


def shards(
    hidden,
    norm_gain,
    query_weight,
    query_bias,
    kv_weight,
    out_weight,
    kv_pool,
    page_table,
    context_len,
):
    slot_count = lax.axis_size(TENSOR)
    section_count = lax.axis_size("section")
    section_id = lax.axis_index("section")
    tensor_id = lax.axis_index(TENSOR)
    row_total, width_dev = hidden.shape
    row_dev = row_total // slot_count
    pool_pages = kv_pool.shape[1]
    gain_row = norm_gain[0].astype(jnp.float32)
    query_proj = query_weight[0]
    bias_row = query_bias[0].astype(jnp.float32)
    kv_proj = kv_weight[0]
    out_proj = out_weight[0]
    pool_layer = kv_pool[0]
    local_pages = page_table - tensor_id * pool_pages
    per_piece = row_dev // row_dev
    tick_count = section_count + row_dev - 1
    is_first = section_id == 0
    finished = [None] * row_dev
    carried = jnp.zeros((slot_count * per_piece, width_dev), jnp.bfloat16)
    for tick_index in range(tick_count):
        if tick_index < row_dev:
            blocks = hidden.reshape(slot_count, row_dev, hidden.shape[1])
            chosen = blocks[:, tick_index * per_piece : (tick_index + 1) * per_piece]
            carried = jnp.where(
                is_first, chosen.reshape(slot_count * per_piece, hidden.shape[1]), carried
            )
        whole = gathered_by_axis(carried, TENSOR, (0, 1), 1)
        wide_rows = whole.astype(jnp.float32)
        mean_sq = jnp.mean(wide_rows * wide_rows, axis=1, keepdims=True)
        normed = (wide_rows * lax.rsqrt(mean_sq + epsilon) * gain_row).astype(jnp.bfloat16)
        queries = (
            jnp.dot(normed, query_proj, preferred_element_type=jnp.float32) + bias_row
        ).astype(jnp.bfloat16)
        fresh_kv = jnp.dot(normed, kv_proj, preferred_element_type=jnp.float32).astype(jnp.bfloat16)
        query_rows = lax.all_to_all(queries, TENSOR, split_axis=0, concat_axis=1, tiled=True)
        fresh_rows = lax.all_to_all(fresh_kv, TENSOR, split_axis=0, concat_axis=1, tiled=True)
        piece_index = jnp.clip(tick_index - section_id, 0, row_dev - 1)
        start_row = piece_index * per_piece
        position = lax.dynamic_slice_in_dim(context_len, start_row, per_piece, 0)
        page_ids = lax.dynamic_slice_in_dim(local_pages, start_row, per_piece, 0)
        cached = pool_layer[page_ids].reshape(per_piece, -1, pool_layer.shape[-1])
        rotated = rotate(
            query_rows.reshape(per_piece, -1, HD).astype(jnp.float32), position
        ).astype(jnp.bfloat16)
        key_new = rotate(
            fresh_rows[:, : KVH * HD].reshape(per_piece, KVH, HD).astype(jnp.float32), position
        ).astype(jnp.bfloat16)
        value_new = fresh_rows[:, KVH * HD :].reshape(per_piece, KVH, HD)
        mixture = attend(rotated, key_new, value_new, cached, position)
        carried = (
            carried.astype(jnp.float32)
            + jnp.dot(
                lax.all_gather(mixture, TENSOR, axis=0, tiled=True),
                out_proj,
                preferred_element_type=jnp.float32,
            )
        ).astype(jnp.bfloat16)
        if tick_index >= section_count - 1:
            finished[tick_index - section_count + 1] = carried
        if tick_index < tick_count - 1:
            carried = shifted(carried, "section", 1)
    stacked = jnp.concatenate(
        [done_part.reshape(slot_count, per_piece, width_dev) for done_part in finished], axis=1
    )
    result = stacked.reshape(row_total, width_dev)
    is_last = section_id == section_count - 1
    outgoing = jnp.where(is_last, result, jnp.zeros_like(result))[None]
    spread = lax.all_to_all(outgoing, "section", split_axis=1, concat_axis=0, tiled=True)
    return spread[section_count - 1]


def solution(mesh):
    finer = Mesh(
        mesh.devices.reshape(mesh.shape["groups"], 16, 2, mesh.shape["section"]),
        ("groups", "tensor_0", "tensor_1", "section"),
    )
    in_specs = (
        P("groups", TENSOR),
        P("section", None),
        P("section", None, TENSOR),
        P("section", TENSOR),
        P("section", None, TENSOR),
        P("section", None, TENSOR),
        P("section", GROUPS_TENSOR, None, None),
        P(GROUPS_TENSOR, None),
        P(GROUPS_TENSOR),
    )
    out_specs = P(("groups", "section"), TENSOR)
    return jax.shard_map(
        shards, mesh=finer, in_specs=in_specs, out_specs=out_specs, check_vma=False
    )
```

profile of v0, /device:TPU:80, one launch (start us, length us, event | category | flops | bytes accessed | tf_op | source)
XLA Modules:
  0.0 1020.4 jit_solution(11074019601654187876)
XLA Ops:
  1.0 69.5 %all-gather = bf16[512,1,256]{2,0,1:T(8,128)(2,1)S(1)} all-gather(bf16[32,1,256]{2,0,1:T(8,128)(2,1)S(1)} %copy_select_fusion), channel_id=2, replica_groups=mesh['groups'=2,'tensor_0'=16,'tensor_1'=2,'section'=8] {'tensor_0'}, dimensions={0}, use_global_device_ids=true | all-gather | bytes 278528 | tf_op jit(solution)/shard_map/all_gather | solution.py:24
  116.3 12.4 %all-to-all-start = ((bf16[32,1,128]{2,1,0:T(2,128)(2,1)}), bf16[32,1,128]{2,1,0:T(2,128)(2,1)S(1)}, u32[]{:S(2)}, u32[]{:S(2)}) async-start(bf16[32,1,128]{2,1,0:T(2,128)(2,1)} %copy.159), calls=%async_computation | async-start | bytes 32768 | tf_op jit(solution)/shard_map/all_to_all | solution.py:136
  129.7 10.8 %all-to-all-done = bf16[32,1,128]{2,1,0:T(2,128)(2,1)S(1)} async-done(((bf16[32,1,128]{2,1,0:T(2,128)(2,1)}), bf16[32,1,128]{2,1,0:T(2,128)(2,1)S(1)}, u32[]{:S(2)}, u32[]{:S(2)}) %all-to-all-start) | async-done | bytes 8224 | tf_op jit(solution)/shard_map/all_to_all | solution.py:136
  141.5 28.8 %all-gather.9 = bf16[32,1,4096]{2,1,0:T(2,128)(2,1)S(1)} all-gather(bf16[1,1,4096]{2,1,0:T(2,128)(2,1)S(1)} %reshape.2331), channel_id=1, replica_groups=mesh['groups'=2,'tensor_0'=16,'tensor_1'=2,'section'=8] {'tensor_0','ten..., dimensions={0}, use_global_device_ids=true | all-gather | bytes 270336 | tf_op jit(solution)/shard_map/all_gather | solution.py:154
  175.8 28.8 %all-gather.1 = bf16[512,256]{1,0:T(8,128)(2,1)S(1)} all-gather(bf16[32,256]{1,0:T(8,128)(2,1)S(1)} %fusion.214), channel_id=3, replica_groups=mesh['groups'=2,'tensor_0'=16,'tensor_1'=2,'section'=8] {'tensor_0'}, dimensions={0}, use_global_device_ids=true | all-gather | bytes 278528 | tf_op jit(solution)/shard_map/all_gather | solution.py:24
  208.4 5.6 all-to-all-start.3
  216.7 9.1 all-to-all-done.3
  230.8 11.4 %all-to-all-done.2 = bf16[32,1,128]{2,1,0:T(2,128)(2,1)S(1)} async-done(((bf16[32,1,128]{2,1,0:T(2,128)(2,1)}), bf16[32,1,128]{2,1,0:T(2,128)(2,1)S(1)}, u32[]{:S(2)}, u32[]{:S(2)}) %all-to-all-start.2) | async-done | bytes 8224 | tf_op jit(solution)/shard_map/all_to_all | solution.py:136
  243.3 28.8 %all-gather.10 = bf16[32,1,4096]{2,1,0:T(2,128)(2,1)S(1)} all-gather(bf16[1,1,4096]{2,1,0:T(2,128)(2,1)S(1)} %reshape.2333), channel_id=1, replica_groups=mesh['groups'=2,'tensor_0'=16,'tensor_1'=2,'section'=8] {'tensor_0','ten..., dimensions={0}, use_global_device_ids=true | all-gather | bytes 270336 | tf_op jit(solution)/shard_map/all_gather | solution.py:154
  278.3 29.3 %all-gather.2 = bf16[512,256]{1,0:T(8,128)(2,1)S(1)} all-gather(bf16[32,256]{1,0:T(8,128)(2,1)S(1)} %collective-permute-done.1), channel_id=4, replica_groups=mesh['groups'=2,'tensor_0'=16,'tensor_1'=2,'section'=8] {'tensor_0'}, dimensions={0}, use_global_device_ids=true | all-gather | bytes 278528 | tf_op jit(solution)/shard_map/all_gather | solution.py:24
  311.4 5.7 all-to-all-start.5
  319.8 9.1 all-to-all-done.5
  333.9 11.4 %all-to-all-done.4 = bf16[32,1,128]{2,1,0:T(2,128)(2,1)S(1)} async-done(((bf16[32,1,128]{2,1,0:T(2,128)(2,1)}), bf16[32,1,128]{2,1,0:T(2,128)(2,1)S(1)}, u32[]{:S(2)}, u32[]{:S(2)}) %all-to-all-start.4) | async-done | bytes 8224 | tf_op jit(solution)/shard_map/all_to_all | solution.py:136
  346.4 28.9 %all-gather.11 = bf16[32,1,4096]{2,1,0:T(2,128)(2,1)S(1)} all-gather(bf16[1,1,4096]{2,1,0:T(2,128)(2,1)S(1)} %reshape.2335), channel_id=1, replica_groups=mesh['groups'=2,'tensor_0'=16,'tensor_1'=2,'section'=8] {'tensor_0','ten..., dimensions={0}, use_global_device_ids=true | all-gather | bytes 270336 | tf_op jit(solution)/shard_map/all_gather | solution.py:154
  381.6 28.7 %all-gather.3 = bf16[512,256]{1,0:T(8,128)(2,1)S(1)} all-gather(bf16[32,256]{1,0:T(8,128)(2,1)S(1)} %collective-permute-done.2), channel_id=5, replica_groups=mesh['groups'=2,'tensor_0'=16,'tensor_1'=2,'section'=8] {'tensor_0'}, dimensions={0}, use_global_device_ids=true | all-gather | bytes 278528 | tf_op jit(solution)/shard_map/all_gather | solution.py:24
  414.1 5.7 all-to-all-start.7
  422.5 9.1 all-to-all-done.7
  436.6 11.4 %all-to-all-done.6 = bf16[32,1,128]{2,1,0:T(2,128)(2,1)S(1)} async-done(((bf16[32,1,128]{2,1,0:T(2,128)(2,1)}), bf16[32,1,128]{2,1,0:T(2,128)(2,1)S(1)}, u32[]{:S(2)}, u32[]{:S(2)}) %all-to-all-start.6) | async-done | bytes 8224 | tf_op jit(solution)/shard_map/all_to_all | solution.py:136
  449.0 28.8 %all-gather.12 = bf16[32,1,4096]{2,1,0:T(2,128)(2,1)S(1)} all-gather(bf16[1,1,4096]{2,1,0:T(2,128)(2,1)S(1)} %reshape.2337), channel_id=1, replica_groups=mesh['groups'=2,'tensor_0'=16,'tensor_1'=2,'section'=8] {'tensor_0','ten..., dimensions={0}, use_global_device_ids=true | all-gather | bytes 270336 | tf_op jit(solution)/shard_map/all_gather | solution.py:154
  484.1 28.8 %all-gather.4 = bf16[512,256]{1,0:T(8,128)(2,1)S(1)} all-gather(bf16[32,256]{1,0:T(8,128)(2,1)S(1)} %collective-permute-done.3), channel_id=6, replica_groups=mesh['groups'=2,'tensor_0'=16,'tensor_1'=2,'section'=8] {'tensor_0'}, dimensions={0}, use_global_device_ids=true | all-gather | bytes 278528 | tf_op jit(solution)/shard_map/all_gather | solution.py:24
  516.8 5.8 all-to-all-start.9
  525.3 9.5 all-to-all-done.9
  539.8 11.4 %all-to-all-done.8 = bf16[32,1,128]{2,1,0:T(2,128)(2,1)S(1)} async-done(((bf16[32,1,128]{2,1,0:T(2,128)(2,1)}), bf16[32,1,128]{2,1,0:T(2,128)(2,1)S(1)}, u32[]{:S(2)}, u32[]{:S(2)}) %all-to-all-start.8) | async-done | bytes 8224 | tf_op jit(solution)/shard_map/all_to_all | solution.py:136
  552.2 28.8 %all-gather.13 = bf16[32,1,4096]{2,1,0:T(2,128)(2,1)S(1)} all-gather(bf16[1,1,4096]{2,1,0:T(2,128)(2,1)S(1)} %reshape.2339), channel_id=1, replica_groups=mesh['groups'=2,'tensor_0'=16,'tensor_1'=2,'section'=8] {'tensor_0','ten..., dimensions={0}, use_global_device_ids=true | all-gather | bytes 270336 | tf_op jit(solution)/shard_map/all_gather | solution.py:154
  587.3 28.8 %all-gather.5 = bf16[512,256]{1,0:T(8,128)(2,1)S(1)} all-gather(bf16[32,256]{1,0:T(8,128)(2,1)S(1)} %collective-permute-done.4), channel_id=7, replica_groups=mesh['groups'=2,'tensor_0'=16,'tensor_1'=2,'section'=8] {'tensor_0'}, dimensions={0}, use_global_device_ids=true | all-gather | bytes 278528 | tf_op jit(solution)/shard_map/all_gather | solution.py:24
  619.9 5.7 all-to-all-start.11
  628.3 9.1 all-to-all-done.11
  642.5 11.4 %all-to-all-done.10 = bf16[32,1,128]{2,1,0:T(2,128)(2,1)S(1)} async-done(((bf16[32,1,128]{2,1,0:T(2,128)(2,1)}), bf16[32,1,128]{2,1,0:T(2,128)(2,1)S(1)}, u32[]{:S(2)}, u32[]{:S(2)}) %all-to-all-start.10) | async-done | bytes 8224 | tf_op jit(solution)/shard_map/all_to_all | solution.py:136
  654.9 28.9 %all-gather.14 = bf16[32,1,4096]{2,1,0:T(2,128)(2,1)S(1)} all-gather(bf16[1,1,4096]{2,1,0:T(2,128)(2,1)S(1)} %reshape.2341), channel_id=1, replica_groups=mesh['groups'=2,'tensor_0'=16,'tensor_1'=2,'section'=8] {'tensor_0','ten..., dimensions={0}, use_global_device_ids=true | all-gather | bytes 270336 | tf_op jit(solution)/shard_map/all_gather | solution.py:154
  684.3 5.6 collective-permute-start.5
  691.3 28.7 %all-gather.6 = bf16[512,256]{1,0:T(8,128)(2,1)S(1)} all-gather(bf16[32,256]{1,0:T(8,128)(2,1)S(1)} %collective-permute-done.5), channel_id=8, replica_groups=mesh['groups'=2,'tensor_0'=16,'tensor_1'=2,'section'=8] {'tensor_0'}, dimensions={0}, use_global_device_ids=true | all-gather | bytes 278528 | tf_op jit(solution)/shard_map/all_gather | solution.py:24
  723.8 5.7 all-to-all-start.13
  732.2 9.1 all-to-all-done.13
  746.3 11.4 %all-to-all-done.12 = bf16[32,1,128]{2,1,0:T(2,128)(2,1)S(1)} async-done(((bf16[32,1,128]{2,1,0:T(2,128)(2,1)}), bf16[32,1,128]{2,1,0:T(2,128)(2,1)S(1)}, u32[]{:S(2)}, u32[]{:S(2)}) %all-to-all-start.12) | async-done | bytes 8224 | tf_op jit(solution)/shard_map/all_to_all | solution.py:136
  758.8 29.1 %all-gather.15 = bf16[32,1,4096]{2,1,0:T(2,128)(2,1)S(1)} all-gather(bf16[1,1,4096]{2,1,0:T(2,128)(2,1)S(1)} %reshape.2343), channel_id=1, replica_groups=mesh['groups'=2,'tensor_0'=16,'tensor_1'=2,'section'=8] {'tensor_0','ten..., dimensions={0}, use_global_device_ids=true | all-gather | bytes 270336 | tf_op jit(solution)/shard_map/all_gather | solution.py:154
  788.4 5.6 collective-permute-start.6
  795.4 28.7 %all-gather.7 = bf16[512,256]{1,0:T(8,128)(2,1)S(1)} all-gather(bf16[32,256]{1,0:T(8,128)(2,1)S(1)} %collective-permute-done.6), channel_id=9, replica_groups=mesh['groups'=2,'tensor_0'=16,'tensor_1'=2,'section'=8] {'tensor_0'}, dimensions={0}, use_global_device_ids=true | all-gather | bytes 278528 | tf_op jit(solution)/shard_map/all_gather | solution.py:24
  827.9 5.7 all-to-all-start.15
  836.3 9.1 all-to-all-done.15
  850.4 11.4 %all-to-all-done.14 = bf16[32,1,128]{2,1,0:T(2,128)(2,1)S(1)} async-done(((bf16[32,1,128]{2,1,0:T(2,128)(2,1)}), bf16[32,1,128]{2,1,0:T(2,128)(2,1)S(1)}, u32[]{:S(2)}, u32[]{:S(2)}) %all-to-all-start.14) | async-done | bytes 8224 | tf_op jit(solution)/shard_map/all_to_all | solution.py:136
  862.8 28.8 %all-gather.16 = bf16[32,1,4096]{2,1,0:T(2,128)(2,1)S(1)} all-gather(bf16[1,1,4096]{2,1,0:T(2,128)(2,1)S(1)} %reshape.2345), channel_id=1, replica_groups=mesh['groups'=2,'tensor_0'=16,'tensor_1'=2,'section'=8] {'tensor_0','ten..., dimensions={0}, use_global_device_ids=true | all-gather | bytes 270336 | tf_op jit(solution)/shard_map/all_gather | solution.py:154
  892.1 5.6 collective-permute-start.7
  899.1 28.8 %all-gather.8 = bf16[512,256]{1,0:T(8,128)(2,1)S(1)} all-gather(bf16[32,256]{1,0:T(8,128)(2,1)S(1)} %collective-permute-done.7), channel_id=10, replica_groups=mesh['groups'=2,'tensor_0'=16,'tensor_1'=2,'section'=8] {'tensor_0'}, dimensions={0}, use_global_device_ids=true | all-gather | bytes 278528 | tf_op jit(solution)/shard_map/all_gather | solution.py:24
  931.7 5.7 all-to-all-start.17
  940.1 9.1 all-to-all-done.17
  954.3 11.4 %all-to-all-done.16 = bf16[32,1,128]{2,1,0:T(2,128)(2,1)S(1)} async-done(((bf16[32,1,128]{2,1,0:T(2,128)(2,1)}), bf16[32,1,128]{2,1,0:T(2,128)(2,1)S(1)}, u32[]{:S(2)}, u32[]{:S(2)}) %all-to-all-start.16) | async-done | bytes 8224 | tf_op jit(solution)/shard_map/all_to_all | solution.py:136
  966.7 28.9 %all-gather.17 = bf16[32,1,4096]{2,1,0:T(2,128)(2,1)S(1)} all-gather(bf16[1,1,4096]{2,1,0:T(2,128)(2,1)S(1)} %reshape.2347), channel_id=1, replica_groups=mesh['groups'=2,'tensor_0'=16,'tensor_1'=2,'section'=8] {'tensor_0','ten..., dimensions={0}, use_global_device_ids=true | all-gather | bytes 270336 | tf_op jit(solution)/shard_map/all_gather | solution.py:154
  997.6 22.0 %all_to_all.273 = bf16[8,2,1024]{2,1,0:T(2,128)(2,1)S(1)} all-to-all(bf16[8,2,1024]{2,1,0:T(2,128)(2,1)S(1)} %reshape.2392), channel_id=1, replica_groups=mesh['groups'=2,'tensor_0'=16,'tensor_1'=2,'section'=8] {'section'}, dimensions={0} | all-to-all | bytes 65536 | tf_op jit(solution)/shard_map/all_to_all | solution.py:169
  (425 shorter events, 181.0 us)
Async XLA Ops:
  0.0 170.2 %copy-start = (bf16[1,4096,256]{2,1,0:T(8,128)(2,1)S(1)}, bf16[1,4096,256]{2,1,0:T(8,128)(2,1)}, u32[]{:S(2)}) copy-start(bf16[1,4096,256]{2,1,0:T(8,128)(2,1)} %param.14) | copy-start | bytes 6291460
  76.7 39.6 %all-to-all-start.1 = ((bf16[32,1,32]{2,1,0:T(2,128)(2,1)}), bf16[32,1,32]{2,1,0:T(2,128)(2,1)}, u32[]{:S(2)}, u32[]{:S(2)}) async-start(bf16[32,1,32]{2,1,0:T(2,128)(2,1)} %copy.161), calls=%async_computation.1 | async-start | bytes 32768 | tf_op jit(solution)/shard_map/all_to_all | solution.py:137
  114.9 60.1 %copy-start.19 = (bf16[1,64,512]{2,1,0:T(8,128)(2,1)S(1)}, bf16[1,64,512]{2,1,0:T(8,128)(2,1)}, u32[]{:S(2)}) copy-start(bf16[1,64,512]{2,1,0:T(8,128)(2,1)} %get-tuple-element.7) | copy-start | bytes 196612
  114.9 60.1 %copy-start.18 = (bf16[1,64,512]{2,1,0:T(8,128)(2,1)S(1)}, bf16[1,64,512]{2,1,0:T(8,128)(2,1)}, u32[]{:S(2)}) copy-start(bf16[1,64,512]{2,1,0:T(8,128)(2,1)} %get-tuple-element.8) | copy-start | bytes 196612
  116.3 24.2 %all-to-all-start = ((bf16[32,1,128]{2,1,0:T(2,128)(2,1)}), bf16[32,1,128]{2,1,0:T(2,128)(2,1)S(1)}, u32[]{:S(2)}, u32[]{:S(2)}) async-start(bf16[32,1,128]{2,1,0:T(2,128)(2,1)} %copy.159), calls=%async_computation | async-start | bytes 32768 | tf_op jit(solution)/shard_map/all_to_all | solution.py:136
  170.8 5.0 collective-permute-start
  208.4 17.4 %all-to-all-start.3 = ((bf16[32,1,32]{2,1,0:T(2,128)(2,1)}), bf16[32,1,32]{2,1,0:T(2,128)(2,1)S(1)}, u32[]{:S(2)}, u32[]{:S(2)}) async-start(bf16[32,1,32]{2,1,0:T(2,128)(2,1)} %copy.167), calls=%async_computation.3 | async-start | bytes 32768 | tf_op jit(solution)/shard_map/all_to_all | solution.py:137
  216.1 61.4 %copy-start.17 = (bf16[1,64,512]{2,1,0:T(8,128)(2,1)S(1)}, bf16[1,64,512]{2,1,0:T(8,128)(2,1)}, u32[]{:S(2)}) copy-start(bf16[1,64,512]{2,1,0:T(8,128)(2,1)} %get-tuple-element.9) | copy-start | bytes 196612
  216.1 61.5 %copy-start.16 = (bf16[1,64,512]{2,1,0:T(8,128)(2,1)S(1)}, bf16[1,64,512]{2,1,0:T(8,128)(2,1)}, u32[]{:S(2)}) copy-start(bf16[1,64,512]{2,1,0:T(8,128)(2,1)} %get-tuple-element.10) | copy-start | bytes 196612
  225.8 16.5 %all-to-all-start.2 = ((bf16[32,1,128]{2,1,0:T(2,128)(2,1)}), bf16[32,1,128]{2,1,0:T(2,128)(2,1)S(1)}, u32[]{:S(2)}, u32[]{:S(2)}) async-start(bf16[32,1,128]{2,1,0:T(2,128)(2,1)} %copy.165), calls=%async_computation.2 | async-start | bytes 32768 | tf_op jit(solution)/shard_map/all_to_all | solution.py:136
  272.5 5.8 collective-permute-start.1
  311.4 17.5 %all-to-all-start.5 = ((bf16[32,1,32]{2,1,0:T(2,128)(2,1)}), bf16[32,1,32]{2,1,0:T(2,128)(2,1)S(1)}, u32[]{:S(2)}, u32[]{:S(2)}) async-start(bf16[32,1,32]{2,1,0:T(2,128)(2,1)} %copy.173), calls=%async_computation.5 | async-start | bytes 32768 | tf_op jit(solution)/shard_map/all_to_all | solution.py:137
  319.2 61.7 %copy-start.15 = (bf16[1,64,512]{2,1,0:T(8,128)(2,1)S(1)}, bf16[1,64,512]{2,1,0:T(8,128)(2,1)}, u32[]{:S(2)}) copy-start(bf16[1,64,512]{2,1,0:T(8,128)(2,1)} %get-tuple-element.11) | copy-start | bytes 196612
  319.2 61.7 %copy-start.14 = (bf16[1,64,512]{2,1,0:T(8,128)(2,1)S(1)}, bf16[1,64,512]{2,1,0:T(8,128)(2,1)}, u32[]{:S(2)}) copy-start(bf16[1,64,512]{2,1,0:T(8,128)(2,1)} %get-tuple-element.12) | copy-start | bytes 196612
  328.9 16.4 %all-to-all-start.4 = ((bf16[32,1,128]{2,1,0:T(2,128)(2,1)}), bf16[32,1,128]{2,1,0:T(2,128)(2,1)S(1)}, u32[]{:S(2)}, u32[]{:S(2)}) async-start(bf16[32,1,128]{2,1,0:T(2,128)(2,1)} %copy.171), calls=%async_computation.4 | async-start | bytes 32768 | tf_op jit(solution)/shard_map/all_to_all | solution.py:136
  375.8 5.8 collective-permute-start.2
  414.1 17.5 %all-to-all-start.7 = ((bf16[32,1,32]{2,1,0:T(2,128)(2,1)}), bf16[32,1,32]{2,1,0:T(2,128)(2,1)S(1)}, u32[]{:S(2)}, u32[]{:S(2)}) async-start(bf16[32,1,32]{2,1,0:T(2,128)(2,1)} %copy.179), calls=%async_computation.7 | async-start | bytes 32768 | tf_op jit(solution)/shard_map/all_to_all | solution.py:137
  421.9 61.4 %copy-start.13 = (bf16[1,64,512]{2,1,0:T(8,128)(2,1)S(1)}, bf16[1,64,512]{2,1,0:T(8,128)(2,1)}, u32[]{:S(2)}) copy-start(bf16[1,64,512]{2,1,0:T(8,128)(2,1)} %get-tuple-element.13) | copy-start | bytes 196612
  421.9 61.4 %copy-start.12 = (bf16[1,64,512]{2,1,0:T(8,128)(2,1)S(1)}, bf16[1,64,512]{2,1,0:T(8,128)(2,1)}, u32[]{:S(2)}) copy-start(bf16[1,64,512]{2,1,0:T(8,128)(2,1)} %get-tuple-element.14) | copy-start | bytes 196612
  431.6 16.4 %all-to-all-start.6 = ((bf16[32,1,128]{2,1,0:T(2,128)(2,1)}), bf16[32,1,128]{2,1,0:T(2,128)(2,1)S(1)}, u32[]{:S(2)}, u32[]{:S(2)}) async-start(bf16[32,1,128]{2,1,0:T(2,128)(2,1)} %copy.177), calls=%async_computation.6 | async-start | bytes 32768 | tf_op jit(solution)/shard_map/all_to_all | solution.py:136
  478.3 5.8 collective-permute-start.3
  515.8 23.8 %copy-start.33 = (f32[64]{0:T(128)S(1)}, f32[64]{0:T(128)}, u32[]{:S(2)}) copy-start(f32[64]{0:T(128)} %get-tuple-element.149) | copy-start | bytes 772
  515.8 23.8 %copy-start.34 = (f32[64]{0:T(128)S(1)}, f32[64]{0:T(128)}, u32[]{:S(2)}) copy-start(f32[64]{0:T(128)} %get-tuple-element.150) | copy-start | bytes 772
  516.8 18.0 %all-to-all-start.9 = ((bf16[32,1,32]{2,1,0:T(2,128)(2,1)}), bf16[32,1,32]{2,1,0:T(2,128)(2,1)S(1)}, u32[]{:S(2)}, u32[]{:S(2)}) async-start(bf16[32,1,32]{2,1,0:T(2,128)(2,1)} %copy.185), calls=%async_computation.9 | async-start | bytes 32768 | tf_op jit(solution)/shard_map/all_to_all | solution.py:137
  524.6 62.0 %copy-start.11 = (bf16[1,64,512]{2,1,0:T(8,128)(2,1)S(1)}, bf16[1,64,512]{2,1,0:T(8,128)(2,1)}, u32[]{:S(2)}) copy-start(bf16[1,64,512]{2,1,0:T(8,128)(2,1)} %get-tuple-element.15) | copy-start | bytes 196612
  524.6 62.0 %copy-start.10 = (bf16[1,64,512]{2,1,0:T(8,128)(2,1)S(1)}, bf16[1,64,512]{2,1,0:T(8,128)(2,1)}, u32[]{:S(2)}) copy-start(bf16[1,64,512]{2,1,0:T(8,128)(2,1)} %get-tuple-element.16) | copy-start | bytes 196612
  534.8 16.4 %all-to-all-start.8 = ((bf16[32,1,128]{2,1,0:T(2,128)(2,1)}), bf16[32,1,128]{2,1,0:T(2,128)(2,1)S(1)}, u32[]{:S(2)}, u32[]{:S(2)}) async-start(bf16[32,1,128]{2,1,0:T(2,128)(2,1)} %copy.183), calls=%async_computation.8 | async-start | bytes 32768 | tf_op jit(solution)/shard_map/all_to_all | solution.py:136
  581.5 5.8 collective-permute-start.4
  619.0 23.3 %copy-start.31 = (f32[64]{0:T(128)S(1)}, f32[64]{0:T(128)}, u32[]{:S(2)}) copy-start(f32[64]{0:T(128)} %get-tuple-element.151) | copy-start | bytes 772
  619.0 23.3 %copy-start.32 = (f32[64]{0:T(128)S(1)}, f32[64]{0:T(128)}, u32[]{:S(2)}) copy-start(f32[64]{0:T(128)} %get-tuple-element.152) | copy-start | bytes 772
  619.9 17.5 %all-to-all-start.11 = ((bf16[32,1,32]{2,1,0:T(2,128)(2,1)}), bf16[32,1,32]{2,1,0:T(2,128)(2,1)S(1)}, u32[]{:S(2)}, u32[]{:S(2)}) async-start(bf16[32,1,32]{2,1,0:T(2,128)(2,1)} %copy.191), calls=%async_computation.11 | async-start | bytes 32768 | tf_op jit(solution)/shard_map/all_to_all | solution.py:137
  627.6 62.9 %copy-start.9 = (bf16[1,64,512]{2,1,0:T(8,128)(2,1)S(1)}, bf16[1,64,512]{2,1,0:T(8,128)(2,1)}, u32[]{:S(2)}) copy-start(bf16[1,64,512]{2,1,0:T(8,128)(2,1)} %get-tuple-element.17) | copy-start | bytes 196612
  627.6 62.9 %copy-start.8 = (bf16[1,64,512]{2,1,0:T(8,128)(2,1)S(1)}, bf16[1,64,512]{2,1,0:T(8,128)(2,1)}, u32[]{:S(2)}) copy-start(bf16[1,64,512]{2,1,0:T(8,128)(2,1)} %get-tuple-element.18) | copy-start | bytes 196612
  637.4 16.5 %all-to-all-start.10 = ((bf16[32,1,128]{2,1,0:T(2,128)(2,1)}), bf16[32,1,128]{2,1,0:T(2,128)(2,1)S(1)}, u32[]{:S(2)}, u32[]{:S(2)}) async-start(bf16[32,1,128]{2,1,0:T(2,128)(2,1)} %copy.189), calls=%async_computation.10 | async-start | bytes 32768 | tf_op jit(solution)/shard_map/all_to_all | solution.py:136
  684.3 7.0 collective-permute-start.5
  723.8 17.5 %all-to-all-start.13 = ((bf16[32,1,32]{2,1,0:T(2,128)(2,1)}), bf16[32,1,32]{2,1,0:T(2,128)(2,1)S(1)}, u32[]{:S(2)}, u32[]{:S(2)}) async-start(bf16[32,1,32]{2,1,0:T(2,128)(2,1)} %copy.197), calls=%async_computation.13 | async-start | bytes 32768 | tf_op jit(solution)/shard_map/all_to_all | solution.py:137
  731.6 63.0 %copy-start.7 = (bf16[1,64,512]{2,1,0:T(8,128)(2,1)S(1)}, bf16[1,64,512]{2,1,0:T(8,128)(2,1)}, u32[]{:S(2)}) copy-start(bf16[1,64,512]{2,1,0:T(8,128)(2,1)} %get-tuple-element.19) | copy-start | bytes 196612
  731.6 63.1 %copy-start.6 = (bf16[1,64,512]{2,1,0:T(8,128)(2,1)S(1)}, bf16[1,64,512]{2,1,0:T(8,128)(2,1)}, u32[]{:S(2)}) copy-start(bf16[1,64,512]{2,1,0:T(8,128)(2,1)} %get-tuple-element.20) | copy-start | bytes 196612
  741.3 16.4 %all-to-all-start.12 = ((bf16[32,1,128]{2,1,0:T(2,128)(2,1)}), bf16[32,1,128]{2,1,0:T(2,128)(2,1)S(1)}, u32[]{:S(2)}, u32[]{:S(2)}) async-start(bf16[32,1,128]{2,1,0:T(2,128)(2,1)} %copy.195), calls=%async_computation.12 | async-start | bytes 32768 | tf_op jit(solution)/shard_map/all_to_all | solution.py:136
  788.4 7.0 collective-permute-start.6
  827.9 17.4 %all-to-all-start.15 = ((bf16[32,1,32]{2,1,0:T(2,128)(2,1)}), bf16[32,1,32]{2,1,0:T(2,128)(2,1)S(1)}, u32[]{:S(2)}, u32[]{:S(2)}) async-start(bf16[32,1,32]{2,1,0:T(2,128)(2,1)} %copy.203), calls=%async_computation.15 | async-start | bytes 32768 | tf_op jit(solution)/shard_map/all_to_all | solution.py:137
  835.6 62.7 %copy-start.5 = (bf16[1,64,512]{2,1,0:T(8,128)(2,1)S(1)}, bf16[1,64,512]{2,1,0:T(8,128)(2,1)}, u32[]{:S(2)}) copy-start(bf16[1,64,512]{2,1,0:T(8,128)(2,1)} %get-tuple-element.21) | copy-start | bytes 196612
  835.6 62.7 %copy-start.4 = (bf16[1,64,512]{2,1,0:T(8,128)(2,1)S(1)}, bf16[1,64,512]{2,1,0:T(8,128)(2,1)}, u32[]{:S(2)}) copy-start(bf16[1,64,512]{2,1,0:T(8,128)(2,1)} %get-tuple-element.22) | copy-start | bytes 196612
  845.4 16.4 %all-to-all-start.14 = ((bf16[32,1,128]{2,1,0:T(2,128)(2,1)}), bf16[32,1,128]{2,1,0:T(2,128)(2,1)S(1)}, u32[]{:S(2)}, u32[]{:S(2)}) async-start(bf16[32,1,128]{2,1,0:T(2,128)(2,1)} %copy.201), calls=%async_computation.14 | async-start | bytes 32768 | tf_op jit(solution)/shard_map/all_to_all | solution.py:136
  892.1 7.0 collective-permute-start.7
  930.8 23.3 %copy-start.25 = (f32[64]{0:T(128)S(1)}, f32[64]{0:T(128)}, u32[]{:S(2)}) copy-start(f32[64]{0:T(128)} %get-tuple-element.157) | copy-start | bytes 772
  931.7 17.5 %all-to-all-start.17 = ((bf16[32,1,32]{2,1,0:T(2,128)(2,1)}), bf16[32,1,32]{2,1,0:T(2,128)(2,1)S(1)}, u32[]{:S(2)}, u32[]{:S(2)}) async-start(bf16[32,1,32]{2,1,0:T(2,128)(2,1)} %copy.209), calls=%async_computation.17 | async-start | bytes 32768 | tf_op jit(solution)/shard_map/all_to_all | solution.py:137
  949.2 16.5 %all-to-all-start.16 = ((bf16[32,1,128]{2,1,0:T(2,128)(2,1)}), bf16[32,1,128]{2,1,0:T(2,128)(2,1)S(1)}, u32[]{:S(2)}, u32[]{:S(2)}) async-start(bf16[32,1,128]{2,1,0:T(2,128)(2,1)} %copy.207), calls=%async_computation.16 | async-start | bytes 32768 | tf_op jit(solution)/shard_map/all_to_all | solution.py:136
  (23 other events, 347.9 us)
where the time goes:
time: 1030 us; the launch traced here: 1020 us
  blocking collectives  602 us (58%)
  waiting for transfers between devices  181 us (18%)
  starting transfers between devices  139 us (13%)
  matrix products  31.6 us (3%)
  other arithmetic  30 us (3%)
  local copies, waits for them, and re-layouts  29.9 us (3%)
    all_gather x18, blocking collectives, all_blocks(): tiles = lax.all_gather(tiles, axes[k], axis=0, tiled=True)  320 us
    all_gather x9, blocking collectives, shards(): lax.all_gather(mixture, TENSOR, axis=0, tiled=True)  260 us
    all_to_all x9, waiting for transfers between devices, shards(): lax.all_to_all(queries, TENSOR, split_axis=0, concat_axis=1, tiled=True)  102 us
    all_to_all x9, waiting for transfers between devices, shards(): lax.all_to_all(fresh_kv, TENSOR, split_axis=0, concat_axis=1, tiled=True)  73.3 us
    all_to_all x9, starting transfers between devices, shards(): lax.all_to_all(fresh_kv, TENSOR, split_axis=0, concat_axis=1, tiled=True)  50.8 us
    all_to_all x9, starting transfers between devices, shards(): lax.all_to_all(queries, TENSOR, split_axis=0, concat_axis=1, tiled=True)  50 us
    ppermute x8, starting transfers between devices, shifted(): lax.ppermute(value, axis, [(source, source + steps) for source in range(i...  37.8 us
    all_to_all x1, blocking collectives, shards(): lax.all_to_all(outgoing, 'section', split_axis=1, concat_axis=0, tiled=True)  22 us
  transfers between devices with their start and end apart: 26, of which 25 were waited for; matrix products, arithmetic and copies ran while one was open for 6% of the time, Pallas kernels for 0%

commit v1 on v0

--- a/solution.py
+++ b/solution.py
@@ -21,7 +21,10 @@
 def all_blocks(shard, axes, turns):
     tiles = shard[None]
     for k in turns:
-        tiles = lax.all_gather(tiles, axes[k], axis=0, tiled=True)
+        view = axes[k]
+        long_array = jnp.stack([tiles] * jax.lax.axis_size(view))
+        carry_out = jax.lax.all_to_all(long_array, view, 0, 0)
+        tiles = jnp.concatenate(carry_out, 0)
     block = [lax.axis_size(axes[k]) for k in reversed(turns)]
     tiles = tiles.reshape(*block, *shard.shape)
     turned = sorted(range(len(turns)), key=lambda place: turns[len(turns) - 1 - place])

time: 1030 us -> 983 us (0.954)
  blocking collectives: 602 us -> 318 us
  waiting for transfers between devices: 181 us -> 334 us
  starting transfers between devices: 139 us -> 222 us
    all_gather x18 -> x0, blocking collectives: 320 us -> none  [all_blocks(): tiles = lax.all_gather(tiles, axes[k], axis=0, tiled=True)]
    all_to_all x0 -> x9, waiting for transfers between devices: none -> 137 us  [all_blocks(): carry_out = jax.lax.all_to_all(long_array, view, 0, 0)]
    all_to_all x0 -> x9, starting transfers between devices: none -> 82.7 us  [all_blocks(): carry_out = jax.lax.all_to_all(long_array, view, 0, 0)]
    all_to_all x0 -> x9, blocking collectives: none -> 37.8 us  [all_blocks(): carry_out = jax.lax.all_to_all(long_array, view, 0, 0)]
  transfers between devices with their start and end apart: 26 -> 35, of which waited for: 25 -> 35; matrix products, arithmetic and copies ran while one was open for 6% -> 5% of each run, Pallas kernels for 0% -> 0%
where the time goes in v1:
time: 983 us; the launch traced here: 972 us
  waiting for transfers between devices  334 us (34%)
  blocking collectives  318 us (32%)
  starting transfers between devices  222 us (23%)
  matrix products  36.7 us (4%)
  local copies, waits for them, and re-layouts  30.3 us (3%)
  other arithmetic  23.2 us (2%)
    all_gather x9, blocking collectives, shards(): lax.all_gather(mixture, TENSOR, axis=0, tiled=True)  260 us
    all_to_all x9, waiting for transfers between devices, all_blocks(): carry_out = jax.lax.all_to_all(long_array, view, 0, 0)  137 us
    all_to_all x9, waiting for transfers between devices, shards(): lax.all_to_all(queries, TENSOR, split_axis=0, concat_axis=1, tiled=True)  103 us
    all_to_all x9, starting transfers between devices, all_blocks(): carry_out = jax.lax.all_to_all(long_array, view, 0, 0)  82.7 us
    all_to_all x9, waiting for transfers between devices, shards(): lax.all_to_all(fresh_kv, TENSOR, split_axis=0, concat_axis=1, tiled=True)  82.7 us
    all_to_all x9, starting transfers between devices, shards(): lax.all_to_all(fresh_kv, TENSOR, split_axis=0, concat_axis=1, tiled=True)  60 us
    all_to_all x9, starting transfers between devices, shards(): lax.all_to_all(queries, TENSOR, split_axis=0, concat_axis=1, tiled=True)  42.9 us
    all_to_all x9, blocking collectives, all_blocks(): carry_out = jax.lax.all_to_all(long_array, view, 0, 0)  37.8 us
  transfers between devices with their start and end apart: 35, of which 35 were waited for; matrix products, arithmetic and copies ran while one was open for 5% of the time, Pallas kernels for 0%

profile of v1, /device:TPU:80, one launch (start us, length us, event | category | flops | bytes accessed | tf_op | source)
XLA Modules:
  0.0 971.6 jit_solution(7299557875515542564)
XLA Ops:
  1.8 43.7 %all-to-all-start = ((bf16[16,1,32,256]{3,2,1,0:T(8,128)(2,1)}), bf16[16,1,32,256]{3,2,1,0:T(8,128)(2,1)S(1)}, u32[]{:S(2)}, u32[]{:S(2)}) async-start(bf16[16,1,32,256]{3,2,1,0:T(8,128)(2,1)} %stack.54), calls=%async_computation | async-start | bytes 524288 | tf_op jit(solution)/shard_map/all_to_all | solution.py:26
  52.3 11.3 %all-to-all-done = bf16[16,1,32,256]{3,2,1,0:T(8,128)(2,1)S(1)} async-done(((bf16[16,1,32,256]{3,2,1,0:T(8,128)(2,1)}), bf16[16,1,32,256]{3,2,1,0:T(8,128)(2,1)S(1)}, u32[]{:S(2)}, u32[]{:S(2)}) %all-to-all-start) | async-done | bytes 262176 | tf_op jit(solution)/shard_map/all_to_all | solution.py:26
  69.3 6.9 all-to-all-start.3
  78.9 9.1 all-to-all-done.3
  93.1 11.4 %all-to-all-done.2 = bf16[32,1,128]{2,1,0:T(2,128)(2,1)S(1)} async-done(((bf16[32,1,128]{2,1,0:T(2,128)(2,1)}), bf16[32,1,128]{2,1,0:T(2,128)(2,1)S(1)}, u32[]{:S(2)}, u32[]{:S(2)}) %all-to-all-start.2) | async-done | bytes 8224 | tf_op jit(solution)/shard_map/all_to_all | solution.py:139
  105.5 28.9 %all-gather = bf16[32,1,4096]{2,1,0:T(2,128)(2,1)S(1)} all-gather(bf16[1,1,4096]{2,1,0:T(2,128)(2,1)S(1)} %reshape.2294), channel_id=1, replica_groups=mesh['groups'=2,'tensor_0'=16,'tensor_1'=2,'section'=8] {'tensor_0','ten..., dimensions={0}, use_global_device_ids=true | all-gather | bytes 270336 | tf_op jit(solution)/shard_map/all_gather | solution.py:157
  148.2 15.3 %all-to-all-done.4 = bf16[16,1,32,256]{3,2,1,0:T(8,128)(2,1)S(1)} async-done(((bf16[16,1,32,256]{3,2,1,0:T(8,128)(2,1)}), bf16[16,1,32,256]{3,2,1,0:T(8,128)(2,1)S(1)}, u32[]{:S(2)}, u32[]{:S(2)}) %all-to-all-start.4) | async-done | bytes 262176 | tf_op jit(solution)/shard_map/all_to_all | solution.py:26
  169.3 6.6 all-to-all-start.7
  178.6 9.1 all-to-all-done.7
  192.8 11.4 %all-to-all-done.6 = bf16[32,1,128]{2,1,0:T(2,128)(2,1)S(1)} async-done(((bf16[32,1,128]{2,1,0:T(2,128)(2,1)}), bf16[32,1,128]{2,1,0:T(2,128)(2,1)S(1)}, u32[]{:S(2)}, u32[]{:S(2)}) %all-to-all-start.6) | async-done | bytes 8224 | tf_op jit(solution)/shard_map/all_to_all | solution.py:139
  207.2 28.9 %all-gather.1 = bf16[32,1,4096]{2,1,0:T(2,128)(2,1)S(1)} all-gather(bf16[1,1,4096]{2,1,0:T(2,128)(2,1)S(1)} %reshape.2296), channel_id=1, replica_groups=mesh['groups'=2,'tensor_0'=16,'tensor_1'=2,'section'=8] {'tensor_0','ten..., dimensions={0}, use_global_device_ids=true | all-gather | bytes 270336 | tf_op jit(solution)/shard_map/all_gather | solution.py:157
  249.6 16.1 %all-to-all-done.8 = bf16[16,1,32,256]{3,2,1,0:T(8,128)(2,1)S(1)} async-done(((bf16[16,1,32,256]{3,2,1,0:T(8,128)(2,1)}), bf16[16,1,32,256]{3,2,1,0:T(8,128)(2,1)S(1)}, u32[]{:S(2)}, u32[]{:S(2)}) %all-to-all-start.8) | async-done | bytes 262176 | tf_op jit(solution)/shard_map/all_to_all | solution.py:26
  271.6 6.6 all-to-all-start.11
  280.9 9.1 all-to-all-done.11
  295.1 11.4 %all-to-all-done.10 = bf16[32,1,128]{2,1,0:T(2,128)(2,1)S(1)} async-done(((bf16[32,1,128]{2,1,0:T(2,128)(2,1)}), bf16[32,1,128]{2,1,0:T(2,128)(2,1)S(1)}, u32[]{:S(2)}, u32[]{:S(2)}) %all-to-all-start.10) | async-done | bytes 8224 | tf_op jit(solution)/shard_map/all_to_all | solution.py:139
  307.5 28.9 %all-gather.2 = bf16[32,1,4096]{2,1,0:T(2,128)(2,1)S(1)} all-gather(bf16[1,1,4096]{2,1,0:T(2,128)(2,1)S(1)} %reshape.2298), channel_id=1, replica_groups=mesh['groups'=2,'tensor_0'=16,'tensor_1'=2,'section'=8] {'tensor_0','ten..., dimensions={0}, use_global_device_ids=true | all-gather | bytes 270336 | tf_op jit(solution)/shard_map/all_gather | solution.py:157
  350.4 15.5 %all-to-all-done.12 = bf16[16,1,32,256]{3,2,1,0:T(8,128)(2,1)S(1)} async-done(((bf16[16,1,32,256]{3,2,1,0:T(8,128)(2,1)}), bf16[16,1,32,256]{3,2,1,0:T(8,128)(2,1)S(1)}, u32[]{:S(2)}, u32[]{:S(2)}) %all-to-all-start.12) | async-done | bytes 262176 | tf_op jit(solution)/shard_map/all_to_all | solution.py:26
  371.7 6.6 all-to-all-start.15
  381.0 9.1 all-to-all-done.15
  395.2 11.4 %all-to-all-done.14 = bf16[32,1,128]{2,1,0:T(2,128)(2,1)S(1)} async-done(((bf16[32,1,128]{2,1,0:T(2,128)(2,1)}), bf16[32,1,128]{2,1,0:T(2,128)(2,1)S(1)}, u32[]{:S(2)}, u32[]{:S(2)}) %all-to-all-start.14) | async-done | bytes 8224 | tf_op jit(solution)/shard_map/all_to_all | solution.py:139
  409.4 28.9 %all-gather.3 = bf16[32,1,4096]{2,1,0:T(2,128)(2,1)S(1)} all-gather(bf16[1,1,4096]{2,1,0:T(2,128)(2,1)S(1)} %reshape.2300), channel_id=1, replica_groups=mesh['groups'=2,'tensor_0'=16,'tensor_1'=2,'section'=8] {'tensor_0','ten..., dimensions={0}, use_global_device_ids=true | all-gather | bytes 270336 | tf_op jit(solution)/shard_map/all_gather | solution.py:157
  451.9 16.0 %all-to-all-done.16 = bf16[16,1,32,256]{3,2,1,0:T(8,128)(2,1)S(1)} async-done(((bf16[16,1,32,256]{3,2,1,0:T(8,128)(2,1)}), bf16[16,1,32,256]{3,2,1,0:T(8,128)(2,1)S(1)}, u32[]{:S(2)}, u32[]{:S(2)}) %all-to-all-start.16) | async-done | bytes 262176 | tf_op jit(solution)/shard_map/all_to_all | solution.py:26
  473.7 6.8 all-to-all-start.19
  483.2 9.6 all-to-all-done.19
  497.8 11.4 %all-to-all-done.18 = bf16[32,1,128]{2,1,0:T(2,128)(2,1)S(1)} async-done(((bf16[32,1,128]{2,1,0:T(2,128)(2,1)}), bf16[32,1,128]{2,1,0:T(2,128)(2,1)S(1)}, u32[]{:S(2)}, u32[]{:S(2)}) %all-to-all-start.18) | async-done | bytes 8224 | tf_op jit(solution)/shard_map/all_to_all | solution.py:139
  510.2 28.9 %all-gather.4 = bf16[32,1,4096]{2,1,0:T(2,128)(2,1)S(1)} all-gather(bf16[1,1,4096]{2,1,0:T(2,128)(2,1)S(1)} %reshape.2302), channel_id=1, replica_groups=mesh['groups'=2,'tensor_0'=16,'tensor_1'=2,'section'=8] {'tensor_0','ten..., dimensions={0}, use_global_device_ids=true | all-gather | bytes 270336 | tf_op jit(solution)/shard_map/all_gather | solution.py:157
  554.2 15.6 %all-to-all-done.20 = bf16[16,1,32,256]{3,2,1,0:T(8,128)(2,1)S(1)} async-done(((bf16[16,1,32,256]{3,2,1,0:T(8,128)(2,1)}), bf16[16,1,32,256]{3,2,1,0:T(8,128)(2,1)S(1)}, u32[]{:S(2)}, u32[]{:S(2)}) %all-to-all-start.20) | async-done | bytes 262176 | tf_op jit(solution)/shard_map/all_to_all | solution.py:26
  575.6 6.6 all-to-all-start.23
  584.9 9.1 all-to-all-done.23
  599.1 11.4 %all-to-all-done.22 = bf16[32,1,128]{2,1,0:T(2,128)(2,1)S(1)} async-done(((bf16[32,1,128]{2,1,0:T(2,128)(2,1)}), bf16[32,1,128]{2,1,0:T(2,128)(2,1)S(1)}, u32[]{:S(2)}, u32[]{:S(2)}) %all-to-all-start.22) | async-done | bytes 8224 | tf_op jit(solution)/shard_map/all_to_all | solution.py:139
  613.4 28.9 %all-gather.5 = bf16[32,1,4096]{2,1,0:T(2,128)(2,1)S(1)} all-gather(bf16[1,1,4096]{2,1,0:T(2,128)(2,1)S(1)} %reshape.2304), channel_id=1, replica_groups=mesh['groups'=2,'tensor_0'=16,'tensor_1'=2,'section'=8] {'tensor_0','ten..., dimensions={0}, use_global_device_ids=true | all-gather | bytes 270336 | tf_op jit(solution)/shard_map/all_gather | solution.py:157
  642.8 5.2 collective-permute-start.5
  657.0 16.0 %all-to-all-done.24 = bf16[16,1,32,256]{3,2,1,0:T(8,128)(2,1)S(1)} async-done(((bf16[16,1,32,256]{3,2,1,0:T(8,128)(2,1)}), bf16[16,1,32,256]{3,2,1,0:T(8,128)(2,1)S(1)}, u32[]{:S(2)}, u32[]{:S(2)}) %all-to-all-start.24) | async-done | bytes 262176 | tf_op jit(solution)/shard_map/all_to_all | solution.py:26
  678.8 6.6 all-to-all-start.27
  688.0 9.1 all-to-all-done.27
  702.3 11.4 %all-to-all-done.26 = bf16[32,1,128]{2,1,0:T(2,128)(2,1)S(1)} async-done(((bf16[32,1,128]{2,1,0:T(2,128)(2,1)}), bf16[32,1,128]{2,1,0:T(2,128)(2,1)S(1)}, u32[]{:S(2)}, u32[]{:S(2)}) %all-to-all-start.26) | async-done | bytes 8224 | tf_op jit(solution)/shard_map/all_to_all | solution.py:139
  714.7 29.3 %all-gather.6 = bf16[32,1,4096]{2,1,0:T(2,128)(2,1)S(1)} all-gather(bf16[1,1,4096]{2,1,0:T(2,128)(2,1)S(1)} %reshape.2306), channel_id=1, replica_groups=mesh['groups'=2,'tensor_0'=16,'tensor_1'=2,'section'=8] {'tensor_0','ten..., dimensions={0}, use_global_device_ids=true | all-gather | bytes 270336 | tf_op jit(solution)/shard_map/all_gather | solution.py:157
  759.3 15.4 %all-to-all-done.28 = bf16[16,1,32,256]{3,2,1,0:T(8,128)(2,1)S(1)} async-done(((bf16[16,1,32,256]{3,2,1,0:T(8,128)(2,1)}), bf16[16,1,32,256]{3,2,1,0:T(8,128)(2,1)S(1)}, u32[]{:S(2)}, u32[]{:S(2)}) %all-to-all-start.28) | async-done | bytes 262176 | tf_op jit(solution)/shard_map/all_to_all | solution.py:26
  780.5 6.6 all-to-all-start.31
  789.8 9.1 all-to-all-done.31
  804.0 11.4 %all-to-all-done.30 = bf16[32,1,128]{2,1,0:T(2,128)(2,1)S(1)} async-done(((bf16[32,1,128]{2,1,0:T(2,128)(2,1)}), bf16[32,1,128]{2,1,0:T(2,128)(2,1)S(1)}, u32[]{:S(2)}, u32[]{:S(2)}) %all-to-all-start.30) | async-done | bytes 8224 | tf_op jit(solution)/shard_map/all_to_all | solution.py:139
  818.4 28.9 %all-gather.7 = bf16[32,1,4096]{2,1,0:T(2,128)(2,1)S(1)} all-gather(bf16[1,1,4096]{2,1,0:T(2,128)(2,1)S(1)} %reshape.2308), channel_id=1, replica_groups=mesh['groups'=2,'tensor_0'=16,'tensor_1'=2,'section'=8] {'tensor_0','ten..., dimensions={0}, use_global_device_ids=true | all-gather | bytes 270336 | tf_op jit(solution)/shard_map/all_gather | solution.py:157
  861.9 16.0 %all-to-all-done.32 = bf16[16,1,32,256]{3,2,1,0:T(8,128)(2,1)S(1)} async-done(((bf16[16,1,32,256]{3,2,1,0:T(8,128)(2,1)}), bf16[16,1,32,256]{3,2,1,0:T(8,128)(2,1)S(1)}, u32[]{:S(2)}, u32[]{:S(2)}) %all-to-all-start.32) | async-done | bytes 262176 | tf_op jit(solution)/shard_map/all_to_all | solution.py:26
  883.8 6.6 all-to-all-start.35
  893.0 9.1 all-to-all-done.35
  907.3 11.4 %all-to-all-done.34 = bf16[32,1,128]{2,1,0:T(2,128)(2,1)S(1)} async-done(((bf16[32,1,128]{2,1,0:T(2,128)(2,1)}), bf16[32,1,128]{2,1,0:T(2,128)(2,1)S(1)}, u32[]{:S(2)}, u32[]{:S(2)}) %all-to-all-start.34) | async-done | bytes 8224 | tf_op jit(solution)/shard_map/all_to_all | solution.py:139
  919.7 28.9 %all-gather.8 = bf16[32,1,4096]{2,1,0:T(2,128)(2,1)S(1)} all-gather(bf16[1,1,4096]{2,1,0:T(2,128)(2,1)S(1)} %reshape.2310), channel_id=1, replica_groups=mesh['groups'=2,'tensor_0'=16,'tensor_1'=2,'section'=8] {'tensor_0','ten..., dimensions={0}, use_global_device_ids=true | all-gather | bytes 270336 | tf_op jit(solution)/shard_map/all_gather | solution.py:157
  950.6 20.3 %all_to_all.372 = bf16[8,2,1024]{2,1,0:T(2,128)(2,1)S(1)} all-to-all(bf16[8,2,1024]{2,1,0:T(2,128)(2,1)S(1)} %reshape.2355), channel_id=1, replica_groups=mesh['groups'=2,'tensor_0'=16,'tensor_1'=2,'section'=8] {'section'}, dimensions={0} | all-to-all | bytes 65536 | tf_op jit(solution)/shard_map/all_to_all | solution.py:172
  (380 shorter events, 252.2 us)
Async XLA Ops:
  0.0 134.4 %copy-start = (bf16[1,4096,256]{2,1,0:T(8,128)(2,1)S(1)}, bf16[1,4096,256]{2,1,0:T(8,128)(2,1)}, u32[]{:S(2)}) copy-start(bf16[1,4096,256]{2,1,0:T(8,128)(2,1)} %param.14) | copy-start | bytes 6291460
  0.0 52.2 %copy-start.9 = (bf16[1,128]{1,0:T(2,128)(2,1)S(1)}, bf16[1,128]{1,0:T(2,128)(2,1)}, u32[]{:S(2)}) copy-start(bf16[1,128]{1,0:T(2,128)(2,1)} %param.12) | copy-start | bytes 772
  1.8 61.8 %all-to-all-start = ((bf16[16,1,32,256]{3,2,1,0:T(8,128)(2,1)}), bf16[16,1,32,256]{3,2,1,0:T(8,128)(2,1)S(1)}, u32[]{:S(2)}, u32[]{:S(2)}) async-start(bf16[16,1,32,256]{3,2,1,0:T(8,128)(2,1)} %stack.54), calls=%async_computation | async-start | bytes 524288 | tf_op jit(solution)/shard_map/all_to_all | solution.py:26
  63.6 4.9 copy-start.1
  69.3 18.7 %all-to-all-start.3 = ((bf16[32,1,32]{2,1,0:T(2,128)(2,1)}), bf16[32,1,32]{2,1,0:T(2,128)(2,1)S(1)}, u32[]{:S(2)}, u32[]{:S(2)}) async-start(bf16[32,1,32]{2,1,0:T(2,128)(2,1)} %copy.113), calls=%async_computation.3 | async-start | bytes 32768 | tf_op jit(solution)/shard_map/all_to_all | solution.py:140
  88.0 16.5 %all-to-all-start.2 = ((bf16[32,1,128]{2,1,0:T(2,128)(2,1)}), bf16[32,1,128]{2,1,0:T(2,128)(2,1)S(1)}, u32[]{:S(2)}, u32[]{:S(2)}) async-start(bf16[32,1,128]{2,1,0:T(2,128)(2,1)} %copy.111), calls=%async_computation.2 | async-start | bytes 32768 | tf_op jit(solution)/shard_map/all_to_all | solution.py:139
  104.8 41.4 %copy-start.2 = (bf16[1,6,16,1024]{3,2,1,0:T(8,128)(2,1)S(1)}, bf16[1,6,16,1024]{3,2,1,0:T(8,128)(2,1)}, u32[]{:S(2)}) copy-start(bf16[1,6,16,1024]{3,2,1,0:T(8,128)(2,1)} %param.15) | copy-start | bytes 589828
  134.9 5.0 collective-permute-start
  140.7 22.9 %all-to-all-start.4 = ((bf16[16,1,32,256]{3,2,1,0:T(8,128)(2,1)}), bf16[16,1,32,256]{3,2,1,0:T(8,128)(2,1)S(1)}, u32[]{:S(2)}, u32[]{:S(2)}) async-start(bf16[16,1,32,256]{3,2,1,0:T(8,128)(2,1)} %stack.56), calls=%async_computation.4 | async-start | bytes 524288 | tf_op jit(solution)/shard_map/all_to_all | solution.py:26
  169.3 18.4 %all-to-all-start.7 = ((bf16[32,1,32]{2,1,0:T(2,128)(2,1)}), bf16[32,1,32]{2,1,0:T(2,128)(2,1)S(1)}, u32[]{:S(2)}, u32[]{:S(2)}) async-start(bf16[32,1,32]{2,1,0:T(2,128)(2,1)} %copy.119), calls=%async_computation.7 | async-start | bytes 32768 | tf_op jit(solution)/shard_map/all_to_all | solution.py:140
  187.8 16.5 %all-to-all-start.6 = ((bf16[32,1,128]{2,1,0:T(2,128)(2,1)}), bf16[32,1,128]{2,1,0:T(2,128)(2,1)S(1)}, u32[]{:S(2)}, u32[]{:S(2)}) async-start(bf16[32,1,128]{2,1,0:T(2,128)(2,1)} %copy.117), calls=%async_computation.6 | async-start | bytes 32768 | tf_op jit(solution)/shard_map/all_to_all | solution.py:139
  236.7 5.4 collective-permute-start.1
  242.8 22.9 %all-to-all-start.8 = ((bf16[16,1,32,256]{3,2,1,0:T(8,128)(2,1)}), bf16[16,1,32,256]{3,2,1,0:T(8,128)(2,1)S(1)}, u32[]{:S(2)}, u32[]{:S(2)}) async-start(bf16[16,1,32,256]{3,2,1,0:T(8,128)(2,1)} %stack.58), calls=%async_computation.8 | async-start | bytes 524288 | tf_op jit(solution)/shard_map/all_to_all | solution.py:26
  271.6 18.4 %all-to-all-start.11 = ((bf16[32,1,32]{2,1,0:T(2,128)(2,1)}), bf16[32,1,32]{2,1,0:T(2,128)(2,1)S(1)}, u32[]{:S(2)}, u32[]{:S(2)}) async-start(bf16[32,1,32]{2,1,0:T(2,128)(2,1)} %copy.125), calls=%async_computation.11 | async-start | bytes 32768 | tf_op jit(solution)/shard_map/all_to_all | solution.py:140
  290.0 16.5 %all-to-all-start.10 = ((bf16[32,1,128]{2,1,0:T(2,128)(2,1)}), bf16[32,1,128]{2,1,0:T(2,128)(2,1)S(1)}, u32[]{:S(2)}, u32[]{:S(2)}) async-start(bf16[32,1,128]{2,1,0:T(2,128)(2,1)} %copy.123), calls=%async_computation.10 | async-start | bytes 32768 | tf_op jit(solution)/shard_map/all_to_all | solution.py:139
  306.5 42.0 %copy-start.7 = (s32[4]{0:T(128)S(1)}, s32[4]{0:T(128)}, u32[]{:S(2)}) copy-start(s32[4]{0:T(128)} %get-tuple-element.102) | copy-start | bytes 52
  306.5 42.0 %copy-start.8 = (s32[4]{0:T(128)S(1)}, s32[4]{0:T(128)}, u32[]{:S(2)}) copy-start(s32[4]{0:T(128)} %get-tuple-element.103) | copy-start | bytes 52
  336.9 5.4 collective-permute-start.2
  343.0 22.9 %all-to-all-start.12 = ((bf16[16,1,32,256]{3,2,1,0:T(8,128)(2,1)}), bf16[16,1,32,256]{3,2,1,0:T(8,128)(2,1)S(1)}, u32[]{:S(2)}, u32[]{:S(2)}) async-start(bf16[16,1,32,256]{3,2,1,0:T(8,128)(2,1)} %stack.60), calls=%async_computation.12 | async-start | bytes 524288 | tf_op jit(solution)/shard_map/all_to_all | solution.py:26
  371.7 18.4 %all-to-all-start.15 = ((bf16[32,1,32]{2,1,0:T(2,128)(2,1)}), bf16[32,1,32]{2,1,0:T(2,128)(2,1)S(1)}, u32[]{:S(2)}, u32[]{:S(2)}) async-start(bf16[32,1,32]{2,1,0:T(2,128)(2,1)} %copy.131), calls=%async_computation.15 | async-start | bytes 32768 | tf_op jit(solution)/shard_map/all_to_all | solution.py:140
  390.1 16.5 %all-to-all-start.14 = ((bf16[32,1,128]{2,1,0:T(2,128)(2,1)}), bf16[32,1,128]{2,1,0:T(2,128)(2,1)S(1)}, u32[]{:S(2)}, u32[]{:S(2)}) async-start(bf16[32,1,128]{2,1,0:T(2,128)(2,1)} %copy.129), calls=%async_computation.14 | async-start | bytes 32768 | tf_op jit(solution)/shard_map/all_to_all | solution.py:139
  438.8 5.5 collective-permute-start.3
  445.0 22.9 %all-to-all-start.16 = ((bf16[16,1,32,256]{3,2,1,0:T(8,128)(2,1)}), bf16[16,1,32,256]{3,2,1,0:T(8,128)(2,1)S(1)}, u32[]{:S(2)}, u32[]{:S(2)}) async-start(bf16[16,1,32,256]{3,2,1,0:T(8,128)(2,1)} %stack.62), calls=%async_computation.16 | async-start | bytes 524288 | tf_op jit(solution)/shard_map/all_to_all | solution.py:26
  473.7 19.0 %all-to-all-start.19 = ((bf16[32,1,32]{2,1,0:T(2,128)(2,1)}), bf16[32,1,32]{2,1,0:T(2,128)(2,1)S(1)}, u32[]{:S(2)}, u32[]{:S(2)}) async-start(bf16[32,1,32]{2,1,0:T(2,128)(2,1)} %copy.137), calls=%async_computation.19 | async-start | bytes 32768 | tf_op jit(solution)/shard_map/all_to_all | solution.py:140
  492.7 16.5 %all-to-all-start.18 = ((bf16[32,1,128]{2,1,0:T(2,128)(2,1)}), bf16[32,1,128]{2,1,0:T(2,128)(2,1)S(1)}, u32[]{:S(2)}, u32[]{:S(2)}) async-start(bf16[32,1,128]{2,1,0:T(2,128)(2,1)} %copy.135), calls=%async_computation.18 | async-start | bytes 32768 | tf_op jit(solution)/shard_map/all_to_all | solution.py:139
  509.2 43.2 %copy-start.5 = (s32[4]{0:T(128)S(1)}, s32[4]{0:T(128)}, u32[]{:S(2)}) copy-start(s32[4]{0:T(128)} %get-tuple-element.100) | copy-start | bytes 52
  509.2 43.2 %copy-start.6 = (s32[4]{0:T(128)S(1)}, s32[4]{0:T(128)}, u32[]{:S(2)}) copy-start(s32[4]{0:T(128)} %get-tuple-element.101) | copy-start | bytes 52
  539.6 6.6 collective-permute-start.4
  547.0 22.9 %all-to-all-start.20 = ((bf16[16,1,32,256]{3,2,1,0:T(8,128)(2,1)}), bf16[16,1,32,256]{3,2,1,0:T(8,128)(2,1)S(1)}, u32[]{:S(2)}, u32[]{:S(2)}) async-start(bf16[16,1,32,256]{3,2,1,0:T(8,128)(2,1)} %stack.64), calls=%async_computation.20 | async-start | bytes 524288 | tf_op jit(solution)/shard_map/all_to_all | solution.py:26
  575.6 18.4 %all-to-all-start.23 = ((bf16[32,1,32]{2,1,0:T(2,128)(2,1)}), bf16[32,1,32]{2,1,0:T(2,128)(2,1)S(1)}, u32[]{:S(2)}, u32[]{:S(2)}) async-start(bf16[32,1,32]{2,1,0:T(2,128)(2,1)} %copy.143), calls=%async_computation.23 | async-start | bytes 32768 | tf_op jit(solution)/shard_map/all_to_all | solution.py:140
  594.0 16.5 %all-to-all-start.22 = ((bf16[32,1,128]{2,1,0:T(2,128)(2,1)}), bf16[32,1,128]{2,1,0:T(2,128)(2,1)S(1)}, u32[]{:S(2)}, u32[]{:S(2)}) async-start(bf16[32,1,128]{2,1,0:T(2,128)(2,1)} %copy.141), calls=%async_computation.22 | async-start | bytes 32768 | tf_op jit(solution)/shard_map/all_to_all | solution.py:139
  642.8 6.6 collective-permute-start.5
  650.1 22.9 %all-to-all-start.24 = ((bf16[16,1,32,256]{3,2,1,0:T(8,128)(2,1)}), bf16[16,1,32,256]{3,2,1,0:T(8,128)(2,1)S(1)}, u32[]{:S(2)}, u32[]{:S(2)}) async-start(bf16[16,1,32,256]{3,2,1,0:T(8,128)(2,1)} %stack.66), calls=%async_computation.24 | async-start | bytes 524288 | tf_op jit(solution)/shard_map/all_to_all | solution.py:26
  678.8 18.4 %all-to-all-start.27 = ((bf16[32,1,32]{2,1,0:T(2,128)(2,1)}), bf16[32,1,32]{2,1,0:T(2,128)(2,1)S(1)}, u32[]{:S(2)}, u32[]{:S(2)}) async-start(bf16[32,1,32]{2,1,0:T(2,128)(2,1)} %copy.149), calls=%async_computation.27 | async-start | bytes 32768 | tf_op jit(solution)/shard_map/all_to_all | solution.py:140
  697.2 16.5 %all-to-all-start.26 = ((bf16[32,1,128]{2,1,0:T(2,128)(2,1)}), bf16[32,1,128]{2,1,0:T(2,128)(2,1)S(1)}, u32[]{:S(2)}, u32[]{:S(2)}) async-start(bf16[32,1,128]{2,1,0:T(2,128)(2,1)} %copy.147), calls=%async_computation.26 | async-start | bytes 32768 | tf_op jit(solution)/shard_map/all_to_all | solution.py:139
  713.7 43.7 %copy-start.3 = (s32[4]{0:T(128)S(1)}, s32[4]{0:T(128)}, u32[]{:S(2)}) copy-start(s32[4]{0:T(128)} %get-tuple-element.98) | copy-start | bytes 52
  713.7 43.7 %copy-start.4 = (s32[4]{0:T(128)S(1)}, s32[4]{0:T(128)}, u32[]{:S(2)}) copy-start(s32[4]{0:T(128)} %get-tuple-element.99) | copy-start | bytes 52
  744.5 6.6 collective-permute-start.6
  751.9 22.9 %all-to-all-start.28 = ((bf16[16,1,32,256]{3,2,1,0:T(8,128)(2,1)}), bf16[16,1,32,256]{3,2,1,0:T(8,128)(2,1)S(1)}, u32[]{:S(2)}, u32[]{:S(2)}) async-start(bf16[16,1,32,256]{3,2,1,0:T(8,128)(2,1)} %stack.68), calls=%async_computation.28 | async-start | bytes 524288 | tf_op jit(solution)/shard_map/all_to_all | solution.py:26
  780.5 18.4 %all-to-all-start.31 = ((bf16[32,1,32]{2,1,0:T(2,128)(2,1)}), bf16[32,1,32]{2,1,0:T(2,128)(2,1)S(1)}, u32[]{:S(2)}, u32[]{:S(2)}) async-start(bf16[32,1,32]{2,1,0:T(2,128)(2,1)} %copy.155), calls=%async_computation.31 | async-start | bytes 32768 | tf_op jit(solution)/shard_map/all_to_all | solution.py:140
  798.9 16.5 %all-to-all-start.30 = ((bf16[32,1,128]{2,1,0:T(2,128)(2,1)}), bf16[32,1,128]{2,1,0:T(2,128)(2,1)S(1)}, u32[]{:S(2)}, u32[]{:S(2)}) async-start(bf16[32,1,128]{2,1,0:T(2,128)(2,1)} %copy.153), calls=%async_computation.30 | async-start | bytes 32768 | tf_op jit(solution)/shard_map/all_to_all | solution.py:139
  847.8 6.6 collective-permute-start.7
  855.1 22.9 %all-to-all-start.32 = ((bf16[16,1,32,256]{3,2,1,0:T(8,128)(2,1)}), bf16[16,1,32,256]{3,2,1,0:T(8,128)(2,1)S(1)}, u32[]{:S(2)}, u32[]{:S(2)}) async-start(bf16[16,1,32,256]{3,2,1,0:T(8,128)(2,1)} %stack.70), calls=%async_computation.32 | async-start | bytes 524288 | tf_op jit(solution)/shard_map/all_to_all | solution.py:26
  883.8 18.4 %all-to-all-start.35 = ((bf16[32,1,32]{2,1,0:T(2,128)(2,1)}), bf16[32,1,32]{2,1,0:T(2,128)(2,1)S(1)}, u32[]{:S(2)}, u32[]{:S(2)}) async-start(bf16[32,1,32]{2,1,0:T(2,128)(2,1)} %copy.161), calls=%async_computation.35 | async-start | bytes 32768 | tf_op jit(solution)/shard_map/all_to_all | solution.py:140
  902.2 16.5 %all-to-all-start.34 = ((bf16[32,1,128]{2,1,0:T(2,128)(2,1)}), bf16[32,1,128]{2,1,0:T(2,128)(2,1)S(1)}, u32[]{:S(2)}, u32[]{:S(2)}) async-start(bf16[32,1,128]{2,1,0:T(2,128)(2,1)} %copy.159), calls=%async_computation.34 | async-start | bytes 32768 | tf_op jit(solution)/shard_map/all_to_all | solution.py:139
